TPU v7x, 256 devices: a whole 4x4x8 slice. The times are simulated.
256 devices in a mesh: pipe: 8 (over x, core), dp: 8 (over z), tensor: 4 (over y).
Axes of the slice: x: 4, y: 4, z: 8, core: 2. Of those that a mesh axis runs over, the one named last changes fastest.
Arguments:
- acts_in: bfloat16 [2, 1024, 4096], P(None, 'dp', 'tensor'), may hold values from -6 to 6
- weights: bfloat16 [8, 4096, 4096], P('pipe', None, 'tensor'), may hold values from -0.046875 to 0.046875
- cotangent: bfloat16 [2, 1024, 4096], P(None, 'dp', 'tensor'), may hold values from -6 to 6
- hist_act: float32 [8, 16], P('pipe'), may hold values from 2 to 12
- hist_weight: float32 [8, 16], P('pipe'), may hold values from 0.01 to 0.1
- hist_grad: float32 [8, 16], P('pipe'), may hold values from 2 to 12
Outputs:
- section_acts: bfloat16 [8, 2, 1024, 4096], P('pipe', None, 'dp', 'tensor')
- section_grads: bfloat16 [8, 2, 1024, 4096], P('pipe', None, 'dp', 'tensor')
- weight_grad: bfloat16 [8, 4096, 4096], P('pipe', 'dp', 'tensor')
- new_hist_act: float32 [8, 16], P('pipe')
- new_hist_weight: float32 [8, 16], P('pipe')
- new_hist_grad: float32 [8, 16], P('pipe')
All inputs are finite; a program needn't handle non-finite values.
Results may differ from a plain program's by a relative error of at most 0.025.
Values may be sent and summed in bfloat16 or wider, within the bound.
A program may use at most 128 MiB of HBM per device.

v0:
```python
import functools

import jax
import jax.numpy as jnp
from jax import lax
from jax.experimental import pallas as pl
from jax.experimental.pallas import tpu as pltpu
from jax.sharding import PartitionSpec as P

MESH = pl.DeviceIdType.MESH
PIECES = 2
WIDE = 1024


def strides_below(index, count):
    low = (index & -index) if index else count
    step, found = low // 2, []
    while step:
        found.append(step)
        step //= 2
    return found


def kernel(S, N, T, NC, RC, F, FA,
           acts, weights, cot, hist_a, hist_w, hist_g,
           out_acts, out_grads, out_w, out_top,
           w, xin, xg, xout, acc, gin, part, rs, gout, G, A, dw, dwb, pk, amax, gmax,
           w_sem, x_ss, x_rs, ag_ss, ag_rs, g_ss, g_rs, rd_ss, rd_rs,
           G_ss, G_rs, A_ss, A_rs, B_ss, B_rs, p_ss, p_rs, o_sem, ow_sem):
    s, d, t = lax.axis_index("pipe"), lax.axis_index("dp"), lax.axis_index("tensor")
    last = S - 1
    bf, f32 = jnp.bfloat16, jnp.float32

    def remote(src, dst, ss, rsem, **where):
        return pltpu.make_async_remote_copy(
            src_ref=src, dst_ref=dst, send_sem=ss, recv_sem=rsem,
            device_id=where, device_id_type=MESH)

    loads = [pltpu.make_async_copy(weights.at[b], w.at[b], w_sem.at[b]) for b in range(T)]
    for copy in loads:
        copy.start()

    barrier = pltpu.get_barrier_semaphore()
    for k in range(N):
        for j in range(T):
            if k or j:
                pl.semaphore_signal(barrier, inc=1, device_id={"dp": d ^ k, "tensor": t ^ j},
                                    device_id_type=MESH)

    @pl.when(s > 0)
    def _():
        pl.semaphore_signal(barrier, inc=1, device_id={"pipe": s - 1}, device_id_type=MESH)

    @pl.when(s < last)
    def _():
        pl.semaphore_signal(barrier, inc=1, device_id={"pipe": s + 1}, device_id_type=MESH)

    lim_a = jnp.max(hist_a[...], axis=1, keepdims=True).astype(bf)
    lim_w = jnp.max(hist_w[...], axis=1, keepdims=True).astype(bf)
    lim_g = jnp.max(hist_g[...], axis=1, keepdims=True).astype(bf)

    def clip(v, lim):
        return jnp.minimum(jnp.maximum(v, -lim), lim)

    def fold(v):
        return jnp.max(jnp.abs(v).reshape(-1, 16, v.shape[-1]), axis=0)

    amax[...] = jnp.zeros_like(amax)
    gmax[...] = jnp.zeros_like(gmax)

    near = (s > 0).astype(jnp.int32) + (s < last).astype(jnp.int32)
    pl.semaphore_wait(barrier, N * T - 1 + near)

    up = jnp.minimum(s + 1, last)
    down = jnp.maximum(s - 1, 0)

    def x_copy(c):
        return remote(xout.at[c], xin.at[c], x_ss.at[c], x_rs.at[c], pipe=up)

    def g_copy(c):
        return remote(gout.at[c], gin.at[c], g_ss.at[c], g_rs.at[c], pipe=down)

    def ag_copy(c, j, st):
        i = j ^ st
        return remote(xg.at[c, j], xg.at[c, i], ag_ss.at[c, i], ag_rs.at[c, i], tensor=t ^ st)

    def low(i):
        return i & -i

    def G_copy(c, j, st):
        i = j ^ st
        return remote(G.at[c, j], G.at[c, i], G_ss.at[c, i], G_rs.at[c, i], dp=d ^ st)

    ratio = N // T

    def in_block(r):
        start = lax.rem(r, ratio) * FA
        return t ^ lax.div(r, ratio), pl.ds(pl.multiple_of(start, FA), FA)

    piece = RC // T

    def rows_of(owner):
        return pl.ds(pl.multiple_of(owner * piece, piece), piece)

    def A_copy(c, k):
        owner, cols = in_block(d ^ k)
        return remote(xg.at[c, owner, rows_of(t), cols], A.at[c, k, rows_of(t)],
                      A_ss.at[c, k], A_rs.at[c, k], dp=d ^ k)

    def B_copy(c, j, st):
        i = j ^ st
        there = A.at[c, pl.ds(1, N - 1), rows_of(t ^ j)]
        return remote(there, there, B_ss.at[c, i], B_rs.at[c, i], tensor=t ^ st)

    def B_arrival(c, i):
        there = A.at[c, pl.ds(1, N - 1), rows_of(t ^ i)]
        return remote(there, there, B_ss.at[c, i], B_rs.at[c, i], tensor=t ^ low(i))

    stages = []
    st = 1
    while st < T:
        stages.append(st)
        st *= 2

    def rd_copy(c, j, level):
        st = stages[level]
        i = j ^ st
        return remote(part.at[c, j], rs.at[c, level, i], rd_ss.at[c, j], rd_rs.at[c, level, i],
                      tensor=t ^ st)

    def prep(c):
        @pl.when(s == 0)
        def _():
            xin[c] = acts[c]

        @pl.when(s > 0)
        def _():
            x_copy(c).wait_recv()

        x = xin[c]
        xg[c, 0] = clip(x, lim_a)
        for st in strides_below(0, T):
            ag_copy(c, 0, st).start()
        amax[...] = jnp.maximum(amax[...], fold(x))

    def clip_weights():
        peak = jnp.zeros((16, F), bf)
        for b in range(T):
            loads[b].wait()

            def body(i, m, b=b):
                rows = pl.ds(pl.multiple_of(i * 128, 128), 128)
                v = w[b, rows]
                w[b, rows] = clip(v, lim_w)
                return jnp.maximum(m, fold(v))

            peak = lax.fori_loop(0, F // 128, body, peak)
        return jnp.max(peak.astype(f32), keepdims=True).reshape(1, 1)

    def compute(c):
        for j in range(T):
            if j:
                ag_copy(c, j ^ low(j), low(j)).wait_recv()
                for st in strides_below(j, T):
                    ag_copy(c, j, st).start()
            b = t ^ j

            def body(n, _, j=j, b=b):
                cols = pl.ds(pl.multiple_of(n * WIDE, WIDE), WIDE)
                y = jnp.dot(xg[c, j], w[b, :, cols], preferred_element_type=f32)
                if j == 0:
                    acc[:, cols] = y
                elif j < T - 1:
                    acc[:, cols] += y
                else:
                    xout[c, :, cols] = (acc[:, cols] + y + xin[c, :, cols].astype(f32)).astype(bf)
                return 0

            lax.fori_loop(0, F // WIDE, body, 0)

        @pl.when(s < last)
        def _():
            x_copy(c).start()

        pltpu.make_async_copy(xout.at[c], out_acts.at[c], o_sem.at[0, c]).start()
        for k in range(1, N):
            A_copy(c, k).start()
        owner, cols = in_block(d)
        A[c, 0] = xg[c, owner, :, cols]

    def prepb(c, is_last):
        if is_last:
            gin[c] = (cot[c].astype(f32) * xout[c].astype(f32)).astype(bf)
        else:
            g_copy(c).wait_recv()
        g = gin[c]
        G[c, 0] = clip(g, lim_g)
        for st in strides_below(0, N):
            G_copy(c, 0, st).start()
        gmax[...] = jnp.maximum(gmax[...], fold(g))
        order = sorted(range(T), key=lambda j: -(low(j) == 1))
        for j in order:
            b = t ^ j

            def body(n, _, j=j, b=b):
                cols = pl.ds(pl.multiple_of(n * WIDE, WIDE), WIDE)
                y = lax.dot_general(G[c, 0], w[b, cols, :], (((1,), (1,)), ((), ())),
                                    preferred_element_type=f32)
                part[c, j, :, cols] = y.astype(bf)
                return 0

            lax.fori_loop(0, F // WIDE, body, 0)
            if low(j) == 1:
                rd_copy(c, j, 0).start()

    def midb(c):
        for level in range(len(stages) - 1):
            st = stages[level]
            js = list(range(0, T, 2 * st))
            for j in sorted(js, key=lambda j: -(low(j) == 2 * st)):
                if j == 0:
                    continue
                rd_copy(c, j ^ st, level).wait_recv()
                part[c, j] = (part[c, j].astype(f32) + rs[c, level, j].astype(f32)).astype(bf)
                if low(j) == 2 * st:
                    rd_copy(c, j, level + 1).start()

    def finb(c):
        total = gin[c].astype(f32) + part[c, 0].astype(f32)
        for level in range(len(stages)):
            rd_copy(c, stages[level], level).wait_recv()
            total = total + rs[c, level, 0].astype(f32)
        gout[c] = total.astype(bf)

        @pl.when(s > 0)
        def _():
            g_copy(c).start()

        pltpu.make_async_copy(gout.at[c], out_grads.at[c], o_sem.at[1, c]).start()

    def relay_G(c):
        for j in range(1, N):
            if strides_below(j, N):
                G_copy(c, j ^ low(j), low(j)).wait_recv()
                for st in strides_below(j, N):
                    G_copy(c, j, st).start()

    def relay_A(c):
        for k in range(1, N):
            A_copy(c, k).wait_recv()
        for st in strides_below(0, T):
            B_copy(c, 0, st).start()

    def relay_B(c):
        for j in range(1, T):
            if strides_below(j, T):
                B_arrival(c, j).wait_recv()
                for st in strides_below(j, T):
                    B_copy(c, j, st).start()

    def update(c):
        for j in range(1, N):
            if not strides_below(j, N):
                G_copy(c, j ^ low(j), low(j)).wait_recv()
        for j in range(1, T):
            if not strides_below(j, T):
                B_arrival(c, j).wait_recv()
        tile = 256

        def body(n, _):
            cols = pl.ds(pl.multiple_of(n * tile, tile), tile)
            y = lax.dot_general(A[c, :, :, cols].reshape(N * RC, tile), G[c].reshape(N * RC, F),
                                (((0,), (0,)), ((), ())), preferred_element_type=f32)
            if c == 0:
                dw[cols, :] = y
            elif c < NC - 1:
                dw[cols, :] += y
            else:
                dwb[cols, :] = (dw[cols, :] + y).astype(bf)
            return 0

        lax.fori_loop(0, FA // tile, body, 0)

    def peers():
        return [(k, j) for k in range(N) for j in range(T) if k or j]

    def p_copy(k, j):
        i = k * T + j
        return remote(pk.at[0], pk.at[i], p_ss.at[i], p_rs.at[i], dp=d ^ k, tensor=t ^ j)

    def send_peaks():
        row = lax.broadcasted_iota(jnp.int32, (8, 128), 0)
        top_a = jnp.max(amax[...].astype(f32), keepdims=True).reshape(1, 1)
        top_g = jnp.max(gmax[...].astype(f32), keepdims=True).reshape(1, 1)
        pk[0] = jnp.where(row == 0, top_a, jnp.where(row == 1, w_peak, top_g))
        for k, j in peers():
            p_copy(k, j).start()

    prep(0)
    if NC > 1:
        prep(1)
    w_peak = clip_weights()

    def backward(i, is_last):
        if i < NC:
            prepb(i, is_last)
            if i == NC - 1:
                send_peaks()
            midb(i)
        if 1 <= i <= NC:
            finb(i - 1)

    @pl.when(s == last)
    def _():
        for c in range(NC):
            compute(c)
            if c + 2 < NC:
                prep(c + 2)
            backward(c, True)
        backward(NC, True)
        for c in range(NC):
            relay_A(c)
            relay_G(c)
        for c in range(NC):
            relay_B(c)
        for c in range(NC - 1):
            update(c)

    @pl.when(s < last)
    def _():
        for c in range(NC):
            compute(c)
            if c + 2 < NC:
                prep(c + 2)
        for c in range(NC):
            relay_A(c)
        for c in range(NC):
            relay_B(c)
        for c in range(NC + 1):
            backward(c, False)
            if c >= 1:
                relay_G(c - 1)
            if c >= 3:
                update(c - 3)
        for c in range(NC - 2, NC - 1):
            update(c)

    update(NC - 1)
    out = pltpu.make_async_copy(dwb, out_w, ow_sem)
    out.start()

    for k, j in peers():
        p_copy(k, j).wait_recv()
    top = jnp.max(pk[...], axis=0)
    out_top[...] = top

    for c in range(NC):
        for i in range(1, T):
            ag_copy(c, i ^ low(i), low(i)).wait_send()
        for level, st in enumerate(stages):
            for j in range(0, T, st):
                if j & st:
                    rd_copy(c, j, level).wait_send()
        for i in range(1, N):
            G_copy(c, i ^ low(i), low(i)).wait_send()
            A_copy(c, i).wait_send()
        for i in range(1, T):
            B_copy(c, i ^ low(i), low(i)).wait_send()
        pltpu.make_async_copy(xout.at[c], out_acts.at[c], o_sem.at[0, c]).wait()
        pltpu.make_async_copy(gout.at[c], out_grads.at[c], o_sem.at[1, c]).wait()

        @pl.when(s < last)
        def _():
            x_copy(c).wait_send()

        @pl.when(s > 0)
        def _():
            g_copy(c).wait_send()

    for k, j in peers():
        p_copy(k, j).wait_send()
    out.wait()


def finish(acts, grads, dw, top, hist_a, hist_w, hist_g,
           out_acts, out_grads, out_w, out_ha, out_hw, out_hg, held_a, held_g, held_w, in_sem, out_sem):
    half = dw.shape[0] // 2
    moves = [(acts, held_a, out_acts.at[0]), (grads, held_g, out_grads.at[0])]
    for i in range(2):
        rows = pl.ds(i * half, half)
        moves.append((dw.at[rows], held_w.at[rows], out_w.at[0, rows]))
    inward = [pltpu.make_async_copy(src, held, in_sem.at[0, i]) for i, (src, held, _) in enumerate(moves)]
    outward = [pltpu.make_async_copy(held, dst, out_sem.at[0, i]) for i, (_, held, dst) in enumerate(moves)]
    for copy in inward:
        copy.start()
    peaks = top[...]
    for row, (hist, out_hist) in enumerate(((hist_a, out_ha), (hist_w, out_hw), (hist_g, out_hg))):
        old = hist[...]
        out_hist[...] = jnp.concatenate([peaks[row:row + 1, 0:1], old[:, :-1]], axis=1)
    for copy, onward in zip(inward, outward):
        copy.wait()
        onward.start()
    for onward in outward:
        onward.wait()


def shards(acts_in, weights, cotangent, hist_act, hist_weight, hist_grad):
    S, N, T = lax.axis_size("pipe"), lax.axis_size("dp"), lax.axis_size("tensor")
    M, R, F = acts_in.shape
    NC, RC = M * PIECES, R // PIECES
    FA = T * F // N
    bf, f32 = jnp.bfloat16, jnp.float32
    levels = max(1, T.bit_length() - 1)
    dma = pltpu.SemaphoreType.DMA
    vmem = pl.BlockSpec(memory_space=pltpu.VMEM)
    anyw = pl.BlockSpec(memory_space=pl.ANY)
    hist = jax.ShapeDtypeStruct(hist_act.shape, f32)
    chunk = (NC, RC, F)
    acts, grads, dw, top = pl.pallas_call(
        functools.partial(kernel, S, N, T, NC, RC, F, FA),
        out_shape=(jax.ShapeDtypeStruct(chunk, bf), jax.ShapeDtypeStruct(chunk, bf),
                   jax.ShapeDtypeStruct((FA, F), bf), jax.ShapeDtypeStruct((8, 128), f32)),
        in_specs=[vmem, anyw, vmem, vmem, vmem, vmem],
        out_specs=(anyw, anyw, anyw, vmem),
        scratch_shapes=[
            pltpu.VMEM((T, F, F), bf),
            pltpu.VMEM(chunk, bf),
            pltpu.VMEM((NC, T, RC, F), bf),
            pltpu.VMEM(chunk, bf),
            pltpu.VMEM((RC, F), f32),
            pltpu.VMEM(chunk, bf),
            pltpu.VMEM((NC, T, RC, F), bf),
            pltpu.VMEM((NC, levels, T, RC, F), bf),
            pltpu.VMEM(chunk, bf),
            pltpu.VMEM((NC, N, RC, F), bf),
            pltpu.VMEM((NC, N, RC, FA), bf),
            pltpu.VMEM((FA, F), f32),
            pltpu.VMEM((FA, F), bf),
            pltpu.VMEM((N * T, 8, 128), f32),
            pltpu.VMEM((16, F), bf),
            pltpu.VMEM((16, F), bf),
            dma((T,)), dma((NC,)), dma((NC,)), dma((NC, T)), dma((NC, T)),
            dma((NC,)), dma((NC,)), dma((NC, T)), dma((NC, levels, T)),
            dma((NC, N)), dma((NC, N)), dma((NC, N)), dma((NC, N)), dma((NC, T)), dma((NC, T)),
            dma((N * T,)), dma((N * T,)), dma((2, NC)), dma(()),
        ],
        compiler_params=pltpu.CompilerParams(
            collective_id=0, has_side_effects=True, vmem_limit_bytes=60 * 2**20),
    )(acts_in.reshape(chunk), weights.reshape(T, F, F), cotangent.reshape(chunk),
      hist_act, hist_weight, hist_grad)
    full = (1, M, R, F)
    return pl.pallas_call(
        finish,
        out_shape=(jax.ShapeDtypeStruct(full, bf), jax.ShapeDtypeStruct(full, bf),
                   jax.ShapeDtypeStruct((1, FA, F), bf), hist, hist, hist),
        in_specs=[anyw, anyw, anyw, vmem, vmem, vmem, vmem],
        out_specs=(anyw, anyw, anyw, vmem, vmem, vmem),
        scratch_shapes=[pltpu.VMEM((M, R, F), bf), pltpu.VMEM((M, R, F), bf),
                        pltpu.VMEM((FA, F), bf), dma((2, 4)), dma((2, 4))],
        compiler_params=pltpu.CompilerParams(vmem_limit_bytes=60 * 2**20),
    )(acts.reshape(M, R, F), grads.reshape(M, R, F), dw, top, hist_act, hist_weight, hist_grad)


def solution(mesh):
    placed = (P(None, "dp", "tensor"), P("pipe", None, "tensor"), P(None, "dp", "tensor"),
              P("pipe", None), P("pipe", None), P("pipe", None))
    return jax.shard_map(
        shards, mesh=mesh, in_specs=placed,
        out_specs=(P("pipe", None, "dp", "tensor"), P("pipe", None, "dp", "tensor"),
                   P("pipe", "dp", "tensor"), P("pipe", None), P("pipe", None), P("pipe", None)),
        check_vma=False)
```

profile of v0, /device:TPU:8, one launch (start us, length us, event | category | flops | bytes accessed | tf_op | source)
XLA Modules:
  0.0 451.7 jit_solution(16193685812842426934)
XLA Ops:
  0.6 447.2 %shard_map.109 = (bf16[4,64,1024]{2,1,0:T(8,128)(2,1)}, bf16[4,64,1024]{2,1,0:T(8,128)(2,1)}, bf16[512,1024]{1,0:T(8,128)(2,1)}, f32[8,128]{1,0:T(8,128)}) custom-call(bf16[4,64,1024]{2,1,0:T(8,128)(2,1)} %bitcast.6, bf16[4,1024,1024]{2,1,0:T(8,128)(2,1)} %bitcast.5, bf16[4,64,1024]{2,1,0:T(8,128)(2,1)} %bitcast.7, f32[1,16]{1,0:T(1,128)} %hist_a.3, ...), custom_call_target="tpu_custom_call" | custom-call | tf_op jit(solution)/shard_map/pallas_call | solution.py:419
  447.8 3.7 shard_map.110
where the time goes:
time: 452 us
  Pallas kernels  451 us (100%)
    pallas_call x1, Pallas kernels, shards(): pl.pallas_call(functools.partial(kernel, S, N, T, NC, RC, F, FA), out_sha...  447 us

commit v1 on v0

v1 whole, which is shorter than its diff:
```python
import functools

import jax
import jax.numpy as jnp
from jax import lax
from jax.experimental import pallas as pl
from jax.experimental.pallas import tpu as pltpu
from jax.sharding import PartitionSpec as P

MESH = pl.DeviceIdType.MESH
PIECES = 4


def kernel(S, N, T, NC, RC, F, FA,
           acts, weights, cot, hist_a, hist_w, hist_g,
           out_acts, out_grads, out_w, out_top,
           w, x, xq, xo, acc, pt, pr, fr, gin, gout, G, A, dw, dwb, pz, py, amax, gmax,
           w_sem, i_ss, x_ss, x_rs, A_ss, A_rs, p_ss, p_rs, f_rs,
           G_ss, G_rs, b_ss, b_rs, z_ss, z_rs, y_ss, y_rs, o_sem, ow_sem):
    s, d, t = lax.axis_index("pipe"), lax.axis_index("dp"), lax.axis_index("tensor")
    last = S - 1
    bf, f32 = jnp.bfloat16, jnp.float32
    late = s >= last - 1
    up = jnp.minimum(s + 1, last)
    down = jnp.maximum(s - 1, 0)
    ratio = N // T
    far_hops = N // 2
    near_hops = N - 1 - far_hops
    offsets = [T // 2] + [o for o in range(1, T) if o != T // 2]

    def remote(src, dst, ss, rsem, **where):
        return pltpu.make_async_remote_copy(
            src_ref=src, dst_ref=dst, send_sem=ss, recv_sem=rsem,
            device_id=where, device_id_type=MESH)

    def peer(o):
        return lax.rem(t + o, T)

    def row(k):
        return lax.rem(d + k, N)

    loads = [pltpu.make_async_copy(weights.at[b], w.at[b], w_sem.at[b]) for b in range(T)]
    for copy in loads:
        copy.start()

    barrier = pltpu.get_barrier_semaphore()
    for k in range(1, N):
        pl.semaphore_signal(barrier, inc=1, device_id={"dp": row(k)}, device_id_type=MESH)
    for o in range(1, T):
        pl.semaphore_signal(barrier, inc=1, device_id={"tensor": peer(o)}, device_id_type=MESH)

    @pl.when(s > 0)
    def _():
        for j in range(T):
            pl.semaphore_signal(barrier, inc=1, device_id={"pipe": s - 1, "tensor": j}, device_id_type=MESH)

    @pl.when(s < last)
    def _():
        for j in range(T):
            pl.semaphore_signal(barrier, inc=1, device_id={"pipe": s + 1, "tensor": j}, device_id_type=MESH)

    lim_a = jnp.max(hist_a[...], axis=1, keepdims=True).astype(bf)
    lim_w = jnp.max(hist_w[...], axis=1, keepdims=True).astype(bf)
    lim_g = jnp.max(hist_g[...], axis=1, keepdims=True).astype(bf)

    def clip(v, lim):
        return jnp.minimum(jnp.maximum(v, -lim), lim)

    def fold(v):
        return jnp.max(jnp.abs(v).reshape(-1, 16, v.shape[-1]), axis=0)

    amax[...] = jnp.zeros_like(amax)
    gmax[...] = jnp.zeros_like(gmax)

    near = (s > 0).astype(jnp.int32) + (s < last).astype(jnp.int32)
    pl.semaphore_wait(barrier, N - 1 + T - 1 + T * near)

    def first_copy(c, o):
        return remote(acts.at[c], x.at[c, t], i_ss.at[c, o], x_rs.at[c, t], tensor=peer(o))

    def x_copy(c, j):
        return remote(xo.at[c], x.at[c, t], x_ss.at[c, j], x_rs.at[c, t], pipe=up, tensor=j)

    def x_arrival(c, j):
        return remote(xo.at[c], x.at[c, j], x_ss.at[c, j], x_rs.at[c, j], pipe=down, tensor=j)

    def block_of(e):
        start = lax.rem(e, ratio) * FA
        return lax.div(e, ratio), pl.ds(pl.multiple_of(start, FA), FA)

    def A_copy(c, k):
        e = row(k)
        b, cols = block_of(e)
        return remote(xq.at[c, b, :, cols], A.at[c, d], A_ss.at[c, k], A_rs.at[c, k], dp=e)

    def A_arrival(c, k):
        r = row(N - k)
        return remote(A.at[c, r], A.at[c, r], A_ss.at[c, k], A_rs.at[c, k], dp=r)

    def p_copy(c, j):
        return remote(pt.at[c, j], pr.at[c, t], p_ss.at[c, j], p_rs.at[c, t], pipe=down, tensor=j)

    def p_arrival(c, j):
        return remote(pt.at[c, j], pr.at[c, j], p_ss.at[c, j], p_rs.at[c, j], pipe=up, tensor=j)

    def f_copy(c, o):
        j = peer(o)
        return remote(pt.at[c, j], fr.at[c, t], p_ss.at[c, j], f_rs.at[c, t], tensor=j)

    def f_arrival(c, o):
        j = peer(o)
        return remote(pt.at[c, j], fr.at[c, j], p_ss.at[c, j], f_rs.at[c, j], tensor=j)

    def back_copy(c):
        return remote(gin.at[c], out_grads.at[c], b_ss.at[c], b_rs.at[c], pipe=up)

    def back_arrival(c):
        return remote(gin.at[c], out_grads.at[c], b_ss.at[c], b_rs.at[c], pipe=down)

    def turn(c):
        return jnp.where(lax.rem(c, 2) == 0, 1, N - 1)

    def G_copy(c, way, h):
        ahead = turn(c) if way == 0 else N - turn(c)
        r = row((h - 1) * (N - ahead))
        return remote(G.at[c, r], G.at[c, r], G_ss.at[c, way, h - 1], G_rs.at[c, way, h - 1],
                      dp=row(ahead))

    def G_arrival(c, way, h):
        ahead = turn(c) if way == 0 else N - turn(c)
        r = row(h * (N - ahead))
        return remote(G.at[c, r], G.at[c, r], G_ss.at[c, way, h - 1], G_rs.at[c, way, h - 1],
                      dp=row(ahead))

    def z_copy(k):
        return remote(pz.at[0], pz.at[k], z_ss.at[k], z_rs.at[k], dp=row(k))

    def y_copy(o):
        return remote(py.at[0], py.at[o], y_ss.at[o], y_rs.at[o], tensor=peer(o))

    def acts_out(c):
        return pltpu.make_async_copy(xo.at[c], out_acts.at[c], o_sem.at[0, c])

    def grads_out(c):
        return pltpu.make_async_copy(gout.at[c], out_grads.at[c], o_sem.at[1, c])

    def each_chunk(body):
        def step(c, _):
            body(c)
            return 0

        lax.fori_loop(0, NC, step, 0)

    @pl.when(s == 0)
    def _():
        def body(c):
            x[c, t] = acts[c]
            for o in offsets:
                first_copy(c, o).start()

        each_chunk(body)

    dw[...] = jnp.zeros_like(dw)

    peak = jnp.zeros((16, F), bf)
    for b in range(T):
        loads[b].wait()

        def squeeze(i, m, b=b):
            rows = pl.ds(pl.multiple_of(i * 128, 128), 128)
            v = w[b, rows]
            w[b, rows] = clip(v, lim_w)
            return jnp.maximum(m, fold(v))

        peak = lax.fori_loop(0, F // 128, squeeze, peak)
    top_w = jnp.max(peak.astype(f32), keepdims=True).reshape(1, 1)
    pz[0] = jnp.broadcast_to(top_w, (8, 128))

    crossing = jnp.logical_and(s > 0, lax.rem(s, 2) == 0)
    middle = [o for o in range(1, T) if o != T // 2]

    def forward(c):
        order = [jnp.where(crossing, T // 2, 0)] + middle + [jnp.where(crossing, 0, T // 2)]
        for k, o in enumerate(order):
            j = peer(o)

            @pl.when(jnp.logical_or(s > 0, j != t))
            def _():
                x_arrival(c, j).wait_recv()

            q = clip(x[c, j], lim_a)
            xq[c, j] = q
            y = jnp.dot(q, w[j], preferred_element_type=f32)
            if k == 0:
                acc[...] = y
            elif k < T - 1:
                acc[...] += y
            else:
                xo[c] = (acc[...] + y + x[c, t].astype(f32)).astype(bf)

        @pl.when(s < last)
        def _():
            for o in offsets + [0]:
                x_copy(c, peer(o)).start()

        acts_out(c).start()
        b, cols = block_of(d)
        A[c, d] = xq[c, b, :, cols]
        amax[...] = jnp.maximum(amax[...], fold(x[c, t]))

        @pl.when(jnp.logical_not(late))
        def _():
            send_A(c)

    def send_A(c):
        for k in range(1, N):
            A_copy(c, k).start()

    def backward(c):
        @pl.when(s == last)
        def _():
            gin[c] = (cot[c].astype(f32) * xo[c].astype(f32)).astype(bf)

        @pl.when(s < last)
        def _():
            for o in range(T):
                p_arrival(c, peer(o)).wait_recv()
            total = pr[c, 0].astype(f32)
            for j in range(1, T):
                total = total + pr[c, j].astype(f32)
            gin[c] = total.astype(bf)
            back_copy(c).start()

        g = gin[c]
        q = clip(g, lim_g)
        G[c, d] = q
        for way in range(2):
            G_copy(c, way, 1).start()
        for o in offsets + [0]:
            b = peer(o)
            y = lax.dot_general(q, w[b], (((1,), (1,)), ((), ())), preferred_element_type=f32)
            if o == 0:
                y = y + g.astype(f32)
            pt[c, b] = y.astype(bf)

            @pl.when(s > 0)
            def _():
                p_copy(c, b).start()

            if o:
                @pl.when(s == 0)
                def _():
                    f_copy(c, o).start()

        gmax[...] = jnp.maximum(gmax[...], fold(g))

        @pl.when(c == NC - 1)
        def _():
            line = lax.broadcasted_iota(jnp.int32, (8, 128), 0)
            top_a = jnp.max(amax[...].astype(f32), keepdims=True).reshape(1, 1)
            top_g = jnp.max(gmax[...].astype(f32), keepdims=True).reshape(1, 1)
            pz[0] = jnp.where(line == 0, top_a, jnp.where(line == 1, pz[0], top_g))
            for k in range(1, N):
                z_copy(k).start()

    def finish_grads(c):
        total = pt[c, t].astype(f32)
        for o in range(1, T):
            f_arrival(c, o).wait_recv()
            total = total + fr[c, peer(o)].astype(f32)
        gout[c] = total.astype(bf)
        grads_out(c).start()

    def relay(c, h):
        @pl.when(jnp.logical_and(c >= 0, c < NC))
        def _():
            for way, hops in ((0, far_hops), (1, near_hops)):
                if h <= hops:
                    G_arrival(c, way, h).wait_recv()
                if h < hops:
                    G_copy(c, way, h + 1).start()

    def update(c):
        for k in range(1, N):
            A_arrival(c, k).wait_recv()
        tile = 256

        def body(n, _):
            cols = pl.ds(pl.multiple_of(n * tile, tile), tile)
            y = lax.dot_general(A[c, :, :, cols].reshape(N * RC, tile), G[c].reshape(N * RC, F),
                                (((0,), (0,)), ((), ())), preferred_element_type=f32)
            y = dw[cols, :] + y
            dw[cols, :] = y
            dwb[cols, :] = y.astype(bf)
            return 0

        lax.fori_loop(0, FA // tile, body, 0)

    def after(c):
        @pl.when(jnp.logical_and(late, c < NC))
        def _():
            send_A(c)

        for h in range(1, far_hops + 1):
            relay(c - h, h)

        @pl.when(jnp.logical_and(s == 0, jnp.logical_and(c >= 1, c <= NC)))
        def _():
            finish_grads(c - 1)

        @pl.when(c == NC + 2)
        def _():
            for k in range(1, N):
                z_copy(k).wait_recv()
            py[0] = jnp.max(pz[...], axis=0)
            for o in range(1, T):
                y_copy(o).start()

        @pl.when(c >= far_hops)
        def _():
            update(c - far_hops)

    def slot(i, _):
        m = i - NC
        is_last = s == last
        even = lax.rem(i, 2) == 0
        half = lax.div(i, 2)
        later = i >= 2 * NC
        paired = m < 2 * NC
        is_fwd = jnp.where(is_last, jnp.logical_and(even, i < 2 * NC), i < NC)
        c_fwd = jnp.where(is_last, half, i)
        early_bwd = jnp.logical_and(jnp.logical_and(m >= 0, paired), lax.rem(m + NC, 2) == NC % 2)
        is_bwd = jnp.where(is_last, jnp.logical_and(jnp.logical_not(even), i < 2 * NC),
                           jnp.where(late, jnp.logical_and(m >= 0, m < NC), early_bwd))
        c_bwd = jnp.where(is_last, half, jnp.where(late, m, lax.div(m, 2)))
        is_after = jnp.logical_and(jnp.logical_not(is_fwd), jnp.logical_not(is_bwd))
        c_after = jnp.where(late, i - 2 * NC, jnp.where(paired, lax.div(m, 2), m - NC))

        @pl.when(is_fwd)
        def _():
            forward(c_fwd)

        @pl.when(is_bwd)
        def _():
            backward(c_bwd)

        @pl.when(is_after)
        def _():
            after(c_after)

        return 0

    lax.fori_loop(0, 3 * NC + far_hops, slot, 0)

    out = pltpu.make_async_copy(dwb, out_w, ow_sem)
    out.start()

    for o in range(1, T):
        y_copy(o).wait_recv()
    out_top[...] = jnp.max(py[...], axis=0)

    def drain(c):
        for k in range(1, N):
            A_copy(c, k).wait_send()
        for way, hops in ((0, far_hops), (1, near_hops)):
            for h in range(1, hops + 1):
                G_copy(c, way, h).wait_send()
        acts_out(c).wait()

        @pl.when(s == 0)
        def _():
            for o in range(1, T):
                first_copy(c, o).wait_send()
                f_copy(c, o).wait_send()
            grads_out(c).wait()

        @pl.when(s > 0)
        def _():
            for j in range(T):
                p_copy(c, j).wait_send()
            back_arrival(c).wait_recv()

        @pl.when(s < last)
        def _():
            for j in range(T):
                x_copy(c, j).wait_send()
            back_copy(c).wait_send()

    each_chunk(drain)
    for k in range(1, N):
        z_copy(k).wait_send()
    for o in range(1, T):
        y_copy(o).wait_send()
    out.wait()


def finish(acts, grads, dw, top, hist_a, hist_w, hist_g,
           out_acts, out_grads, out_w, out_ha, out_hw, out_hg, held_a, held_g, held_w, in_sem, out_sem):
    half = dw.shape[0] // 2
    moves = [(acts, held_a, out_acts.at[0]), (grads, held_g, out_grads.at[0])]
    for i in range(2):
        rows = pl.ds(i * half, half)
        moves.append((dw.at[rows], held_w.at[rows], out_w.at[0, rows]))
    inward = [pltpu.make_async_copy(src, held, in_sem.at[0, i]) for i, (src, held, _) in enumerate(moves)]
    outward = [pltpu.make_async_copy(held, dst, out_sem.at[0, i]) for i, (_, held, dst) in enumerate(moves)]
    for copy in inward:
        copy.start()
    peaks = top[...]
    for row, (hist, out_hist) in enumerate(((hist_a, out_ha), (hist_w, out_hw), (hist_g, out_hg))):
        old = hist[...]
        out_hist[...] = jnp.concatenate([peaks[row:row + 1, 0:1], old[:, :-1]], axis=1)
    for copy, onward in zip(inward, outward):
        copy.wait()
        onward.start()
    for onward in outward:
        onward.wait()


def shards(acts_in, weights, cotangent, hist_act, hist_weight, hist_grad):
    S, N, T = lax.axis_size("pipe"), lax.axis_size("dp"), lax.axis_size("tensor")
    M, R, F = acts_in.shape
    NC, RC = M * PIECES, R // PIECES
    FA = T * F // N
    bf, f32 = jnp.bfloat16, jnp.float32
    dma = pltpu.SemaphoreType.DMA
    vmem = pl.BlockSpec(memory_space=pltpu.VMEM)
    anyw = pl.BlockSpec(memory_space=pl.ANY)
    hist = jax.ShapeDtypeStruct(hist_act.shape, f32)
    chunk = (NC, RC, F)
    acts, grads, dw, top = pl.pallas_call(
        functools.partial(kernel, S, N, T, NC, RC, F, FA),
        out_shape=(jax.ShapeDtypeStruct(chunk, bf), jax.ShapeDtypeStruct(chunk, bf),
                   jax.ShapeDtypeStruct((FA, F), bf), jax.ShapeDtypeStruct((8, 128), f32)),
        in_specs=[vmem, anyw, vmem, vmem, vmem, vmem],
        out_specs=(anyw, anyw, anyw, vmem),
        scratch_shapes=[
            pltpu.VMEM((T, F, F), bf),
            pltpu.VMEM((NC, T, RC, F), bf),
            pltpu.VMEM((NC, T, RC, F), bf),
            pltpu.VMEM(chunk, bf),
            pltpu.VMEM((RC, F), f32),
            pltpu.VMEM((NC, T, RC, F), bf),
            pltpu.VMEM((NC, T, RC, F), bf),
            pltpu.VMEM((NC, T, RC, F), bf),
            pltpu.VMEM(chunk, bf),
            pltpu.VMEM(chunk, bf),
            pltpu.VMEM((NC, N, RC, F), bf),
            pltpu.VMEM((NC, N, RC, FA), bf),
            pltpu.VMEM((FA, F), f32),
            pltpu.VMEM((FA, F), bf),
            pltpu.VMEM((N, 8, 128), f32),
            pltpu.VMEM((T, 8, 128), f32),
            pltpu.VMEM((16, F), bf),
            pltpu.VMEM((16, F), bf),
            dma((T,)), dma((NC, T)), dma((NC, T)), dma((NC, T)), dma((NC, N)), dma((NC, N)),
            dma((NC, T)), dma((NC, T)), dma((NC, T)),
            dma((NC, 2, N // 2)), dma((NC, 2, N // 2)), dma((NC,)), dma((NC,)),
            dma((N,)), dma((N,)), dma((T,)), dma((T,)), dma((2, NC)), dma(()),
        ],
        compiler_params=pltpu.CompilerParams(
            collective_id=0, has_side_effects=True, vmem_limit_bytes=60 * 2**20),
    )(acts_in.reshape(chunk), weights.reshape(T, F, F), cotangent.reshape(chunk),
      hist_act, hist_weight, hist_grad)
    full = (1, M, R, F)
    return pl.pallas_call(
        finish,
        out_shape=(jax.ShapeDtypeStruct(full, bf), jax.ShapeDtypeStruct(full, bf),
                   jax.ShapeDtypeStruct((1, FA, F), bf), hist, hist, hist),
        in_specs=[anyw, anyw, anyw, vmem, vmem, vmem, vmem],
        out_specs=(anyw, anyw, anyw, vmem, vmem, vmem),
        scratch_shapes=[pltpu.VMEM((M, R, F), bf), pltpu.VMEM((M, R, F), bf),
                        pltpu.VMEM((FA, F), bf), dma((2, 4)), dma((2, 4))],
        compiler_params=pltpu.CompilerParams(vmem_limit_bytes=60 * 2**20),
    )(acts.reshape(M, R, F), grads.reshape(M, R, F), dw, top, hist_act, hist_weight, hist_grad)


def solution(mesh):
    placed = (P(None, "dp", "tensor"), P("pipe", None, "tensor"), P(None, "dp", "tensor"),
              P("pipe", None), P("pipe", None), P("pipe", None))
    return jax.shard_map(
        shards, mesh=mesh, in_specs=placed,
        out_specs=(P("pipe", None, "dp", "tensor"), P("pipe", None, "dp", "tensor"),
                   P("pipe", "dp", "tensor"), P("pipe", None), P("pipe", None), P("pipe", None)),
        check_vma=False)
```

time: 452 us -> 192 us (0.42)
  the two profiles are of different devices: /device:TPU:8 before, /device:TPU:6 now
where the time goes in v1:
time: 192 us
  Pallas kernels  191 us (99%)
    pallas_call x1, Pallas kernels, shards(): pl.pallas_call(functools.partial(kernel, S, N, T, NC, RC, F, FA), out_sha...  187 us

profile of v1, /device:TPU:6, one launch (start us, length us, event | category | flops | bytes accessed | tf_op | source)
XLA Modules:
  0.0 191.7 jit_solution(4485467888485354145)
XLA Ops:
  0.6 187.4 %shard_map.109 = (bf16[8,32,1024]{2,1,0:T(8,128)(2,1)}, bf16[8,32,1024]{2,1,0:T(8,128)(2,1)}, bf16[512,1024]{1,0:T(8,128)(2,1)}, f32[8,128]{1,0:T(8,128)}) custom-call(bf16[8,32,1024]{2,1,0:T(8,128)(2,1)} %bitcast.6, bf16[4,1024,1024]{2,1,0:T(8,128)(2,1)} %bitcast.5, bf16[8,32,1024]{2,1,0:T(8,128)(2,1)} %bitcast.7, f32[1,16]{1,0:T(1,128)} %hist_a.3, ...), custom_call_target="tpu_custom_call" | custom-call | tf_op jit(solution)/shard_map/pallas_call | solution.py:430
  188.0 3.7 %shard_map.110 = (bf16[1,2,128,1024]{3,2,1,0:T(8,128)(2,1)}, bf16[1,2,128,1024]{3,2,1,0:T(8,128)(2,1)}, bf16[1,512,1024]{2,1,0:T(8,128)(2,1)}, f32[1,16]{1,0:T(1...) custom-call(bf16[2,128,1024]{2,1,0:T(8,128)(2,1)} %bitcast.8, bf16[2,128,1024]{2,1,0:T(8,128)(2,1)} %bitcast.9, ...), custom_call_target="tpu_custom_call" | custom-call | tf_op jit(solution)/shard_map/pallas_call | solution.py:465

commit v2 on v1

--- a/solution.py
+++ b/solution.py
@@ -9,18 +9,22 @@
 
 MESH = pl.DeviceIdType.MESH
 PIECES = 4
+AHEAD = 4
+LAG = 2
+GROUP = 4
 
 
 def kernel(S, N, T, NC, RC, F, FA,
            acts, weights, cot, hist_a, hist_w, hist_g,
            out_acts, out_grads, out_w, out_top,
-           w, x, xq, xo, acc, pt, pr, fr, gin, gout, G, A, dw, dwb, pz, py, amax, gmax,
-           w_sem, i_ss, x_ss, x_rs, A_ss, A_rs, p_ss, p_rs, f_rs,
+           w, wt, x, xq, xo, acc, pt, pr, gin, gout, G, A, dw, dwb, pz, py, amax, gmax,
+           w_sem, i_ss, x_ss, x_rs, A_ss, A_rs, p_ss, p_rs,
            G_ss, G_rs, b_ss, b_rs, z_ss, z_rs, y_ss, y_rs, o_sem, ow_sem):
     s, d, t = lax.axis_index("pipe"), lax.axis_index("dp"), lax.axis_index("tensor")
     last = S - 1
     bf, f32 = jnp.bfloat16, jnp.float32
-    late = s >= last - 1
+    late = s >= S // 2
+    level = (s == 0).astype(jnp.int32)
     up = jnp.minimum(s + 1, last)
     down = jnp.maximum(s - 1, 0)
     ratio = N // T
@@ -98,18 +102,14 @@
         return remote(A.at[c, r], A.at[c, r], A_ss.at[c, k], A_rs.at[c, k], dp=r)
 
     def p_copy(c, j):
-        return remote(pt.at[c, j], pr.at[c, t], p_ss.at[c, j], p_rs.at[c, t], pipe=down, tensor=j)
+        return remote(pt.at[c, j], pr.at[level, c, t], p_ss.at[c, j], p_rs.at[level, c, t],
+                      pipe=down, tensor=j)
 
     def p_arrival(c, j):
-        return remote(pt.at[c, j], pr.at[c, j], p_ss.at[c, j], p_rs.at[c, j], pipe=up, tensor=j)
-
-    def f_copy(c, o):
-        j = peer(o)
-        return remote(pt.at[c, j], fr.at[c, t], p_ss.at[c, j], f_rs.at[c, t], tensor=j)
-
-    def f_arrival(c, o):
-        j = peer(o)
-        return remote(pt.at[c, j], fr.at[c, j], p_ss.at[c, j], f_rs.at[c, j], tensor=j)
+        return remote(pt.at[c, j], pr.at[0, c, j], p_ss.at[c, j], p_rs.at[0, c, j], pipe=up, tensor=j)
+
+    def f_arrival(c, j):
+        return remote(pt.at[c, j], pr.at[1, c, j], p_ss.at[c, j], p_rs.at[1, c, j], tensor=j)
 
     def back_copy(c):
         return remote(gin.at[c], out_grads.at[c], b_ss.at[c], b_rs.at[c], pipe=up)
@@ -151,16 +151,19 @@
 
         lax.fori_loop(0, NC, step, 0)
 
+    def send_first(c):
+        for o in offsets:
+            first_copy(c, o).start()
+
     @pl.when(s == 0)
     def _():
+        for c in range(AHEAD):
+            send_first(c)
+
         def body(c):
             x[c, t] = acts[c]
-            for o in offsets:
-                first_copy(c, o).start()
 
         each_chunk(body)
-
-    dw[...] = jnp.zeros_like(dw)
 
     peak = jnp.zeros((16, F), bf)
     for b in range(T):
@@ -176,42 +179,55 @@
     top_w = jnp.max(peak.astype(f32), keepdims=True).reshape(1, 1)
     pz[0] = jnp.broadcast_to(top_w, (8, 128))
 
+    def flip_weights():
+        def turn_block(i, _):
+            b, n = lax.div(i, F // 128), lax.rem(i, F // 128)
+            rows = pl.ds(pl.multiple_of(n * 128, 128), 128)
+            wt[b, :, rows] = w[b, rows, :].T
+            return 0
+
+        lax.fori_loop(0, T * (F // 128), turn_block, 0)
+
+    pl.when(late)(flip_weights)
+
     crossing = jnp.logical_and(s > 0, lax.rem(s, 2) == 0)
     middle = [o for o in range(1, T) if o != T // 2]
 
     def forward(c):
-        order = [jnp.where(crossing, T // 2, 0)] + middle + [jnp.where(crossing, 0, T // 2)]
-        for k, o in enumerate(order):
-            j = peer(o)
-
-            @pl.when(jnp.logical_or(s > 0, j != t))
-            def _():
-                x_arrival(c, j).wait_recv()
-
+        first = peer(jnp.where(crossing, T // 2, 0))
+        rest = [peer(o) for o in middle] + [peer(jnp.where(crossing, 0, T // 2))]
+
+        @pl.when(s > 0)
+        def _():
+            x_arrival(c, first).wait_recv()
+
+        q = clip(x[c, first], lim_a)
+        xq[c, first] = q
+        acc[...] = jnp.dot(q, w[first], preferred_element_type=f32)
+        for j in rest:
+            x_arrival(c, j).wait_recv()
+        y = acc[...] + x[c, t].astype(f32)
+        for j in rest:
             q = clip(x[c, j], lim_a)
             xq[c, j] = q
-            y = jnp.dot(q, w[j], preferred_element_type=f32)
-            if k == 0:
-                acc[...] = y
-            elif k < T - 1:
-                acc[...] += y
-            else:
-                xo[c] = (acc[...] + y + x[c, t].astype(f32)).astype(bf)
+            y = y + jnp.dot(q, w[j], preferred_element_type=f32)
+        xo[c] = y.astype(bf)
 
         @pl.when(s < last)
         def _():
             for o in offsets + [0]:
                 x_copy(c, peer(o)).start()
 
+        @pl.when(jnp.logical_and(s == 0, c + AHEAD < NC))
+        def _():
+            send_first(jnp.minimum(c + AHEAD, NC - 1))
+
         acts_out(c).start()
+        send_A(c)
         b, cols = block_of(d)
         A[c, d] = xq[c, b, :, cols]
         amax[...] = jnp.maximum(amax[...], fold(x[c, t]))
 
-        @pl.when(jnp.logical_not(late))
-        def _():
-            send_A(c)
-
     def send_A(c):
         for k in range(1, N):
             A_copy(c, k).start()
@@ -225,9 +241,9 @@
         def _():
             for o in range(T):
                 p_arrival(c, peer(o)).wait_recv()
-            total = pr[c, 0].astype(f32)
+            total = pr[0, c, 0].astype(f32)
             for j in range(1, T):
-                total = total + pr[c, j].astype(f32)
+                total = total + pr[0, c, j].astype(f32)
             gin[c] = total.astype(bf)
             back_copy(c).start()
 
@@ -236,21 +252,16 @@
         G[c, d] = q
         for way in range(2):
             G_copy(c, way, 1).start()
-        for o in offsets + [0]:
+        for o in offsets:
             b = peer(o)
-            y = lax.dot_general(q, w[b], (((1,), (1,)), ((), ())), preferred_element_type=f32)
-            if o == 0:
-                y = y + g.astype(f32)
-            pt[c, b] = y.astype(bf)
-
-            @pl.when(s > 0)
-            def _():
-                p_copy(c, b).start()
-
-            if o:
-                @pl.when(s == 0)
-                def _():
-                    f_copy(c, o).start()
+            pt[c, b] = jnp.dot(q, wt[b], preferred_element_type=f32).astype(bf)
+            p_copy(c, b).start()
+        y = jnp.dot(q, wt[t], preferred_element_type=f32) + g.astype(f32)
+        pt[c, t] = y.astype(bf)
+
+        @pl.when(s > 0)
+        def _():
+            p_copy(c, t).start()
 
         gmax[...] = jnp.maximum(gmax[...], fold(g))
 
@@ -266,8 +277,8 @@
     def finish_grads(c):
         total = pt[c, t].astype(f32)
         for o in range(1, T):
-            f_arrival(c, o).wait_recv()
-            total = total + fr[c, peer(o)].astype(f32)
+            f_arrival(c, peer(o)).wait_recv()
+            total = total + pr[1, c, peer(o)].astype(f32)
         gout[c] = total.astype(bf)
         grads_out(c).start()
 
@@ -280,29 +291,33 @@
                 if h < hops:
                     G_copy(c, way, h + 1).start()
 
-    def update(c):
-        for k in range(1, N):
-            A_arrival(c, k).wait_recv()
-        tile = 256
+    def update(first):
+        def arrived(c, _):
+            for k in range(1, N):
+                A_arrival(c, k).wait_recv()
+            return 0
+
+        lax.fori_loop(first, first + GROUP, arrived, 0)
+        tile, depth = 256, GROUP * N * RC
+        span = pl.ds(first, GROUP)
 
         def body(n, _):
             cols = pl.ds(pl.multiple_of(n * tile, tile), tile)
-            y = lax.dot_general(A[c, :, :, cols].reshape(N * RC, tile), G[c].reshape(N * RC, F),
+            y = lax.dot_general(A[span, :, :, cols].reshape(depth, tile), G[span].reshape(depth, F),
                                 (((0,), (0,)), ((), ())), preferred_element_type=f32)
-            y = dw[cols, :] + y
-            dw[cols, :] = y
-            dwb[cols, :] = y.astype(bf)
+            if first:
+                y = dw[cols, :] + y
+            if first + GROUP < NC:
+                dw[cols, :] = y
+            else:
+                dwb[cols, :] = y.astype(bf)
             return 0
 
         lax.fori_loop(0, FA // tile, body, 0)
 
     def after(c):
-        @pl.when(jnp.logical_and(late, c < NC))
-        def _():
-            send_A(c)
-
         for h in range(1, far_hops + 1):
-            relay(c - h, h)
+            relay(c - LAG * h, h)
 
         @pl.when(jnp.logical_and(s == 0, jnp.logical_and(c >= 1, c <= NC)))
         def _():
@@ -316,9 +331,10 @@
             for o in range(1, T):
                 y_copy(o).start()
 
-        @pl.when(c >= far_hops)
-        def _():
-            update(c - far_hops)
+        for first in range(0, NC, GROUP):
+            @pl.when(c == first + GROUP - 1 + LAG * far_hops)
+            def _():
+                update(first)
 
     def slot(i, _):
         m = i - NC
@@ -336,6 +352,10 @@
         is_after = jnp.logical_and(jnp.logical_not(is_fwd), jnp.logical_not(is_bwd))
         c_after = jnp.where(late, i - 2 * NC, jnp.where(paired, lax.div(m, 2), m - NC))
 
+        @pl.when(jnp.logical_and(i == NC, jnp.logical_not(late)))
+        def _():
+            flip_weights()
+
         @pl.when(is_fwd)
         def _():
             forward(c_fwd)
@@ -350,7 +370,7 @@
 
         return 0
 
-    lax.fori_loop(0, 3 * NC + far_hops, slot, 0)
+    lax.fori_loop(0, 3 * NC + LAG * far_hops, slot, 0)
 
     out = pltpu.make_async_copy(dwb, out_w, ow_sem)
     out.start()
@@ -366,18 +386,18 @@
             for h in range(1, hops + 1):
                 G_copy(c, way, h).wait_send()
         acts_out(c).wait()
+        for o in range(1, T):
+            p_copy(c, peer(o)).wait_send()
 
         @pl.when(s == 0)
         def _():
             for o in range(1, T):
                 first_copy(c, o).wait_send()
-                f_copy(c, o).wait_send()
             grads_out(c).wait()
 
         @pl.when(s > 0)
         def _():
-            for j in range(T):
-                p_copy(c, j).wait_send()
+            p_copy(c, t).wait_send()
             back_arrival(c).wait_recv()
 
         @pl.when(s < last)
@@ -435,13 +455,13 @@
         out_specs=(anyw, anyw, anyw, vmem),
         scratch_shapes=[
             pltpu.VMEM((T, F, F), bf),
+            pltpu.VMEM((T, F, F), bf),
             pltpu.VMEM((NC, T, RC, F), bf),
             pltpu.VMEM((NC, T, RC, F), bf),
             pltpu.VMEM(chunk, bf),
             pltpu.VMEM((RC, F), f32),
             pltpu.VMEM((NC, T, RC, F), bf),
-            pltpu.VMEM((NC, T, RC, F), bf),
-            pltpu.VMEM((NC, T, RC, F), bf),
+            pltpu.VMEM((2, NC, T, RC, F), bf),
             pltpu.VMEM(chunk, bf),
             pltpu.VMEM(chunk, bf),
             pltpu.VMEM((NC, N, RC, F), bf),
@@ -453,7 +473,7 @@
             pltpu.VMEM((16, F), bf),
             pltpu.VMEM((16, F), bf),
             dma((T,)), dma((NC, T)), dma((NC, T)), dma((NC, T)), dma((NC, N)), dma((NC, N)),
-            dma((NC, T)), dma((NC, T)), dma((NC, T)),
+            dma((NC, T)), dma((2, NC, T)),
             dma((NC, 2, N // 2)), dma((NC, 2, N // 2)), dma((NC,)), dma((NC,)),
             dma((N,)), dma((N,)), dma((T,)), dma((T,)), dma((2, NC)), dma(()),
         ],

time: 192 us -> 169 us (0.88)
  the two profiles are of different devices: /device:TPU:6 before, /device:TPU:8 now
where the time goes in v2:
time: 169 us
  Pallas kernels  168 us (99%)
    pallas_call x1, Pallas kernels, shards(): pl.pallas_call(functools.partial(kernel, S, N, T, NC, RC, F, FA), out_sha...  164 us
    pallas_call x1, Pallas kernels, shards(): pl.pallas_call(finish, out_shape=(jax.ShapeDtypeStruct(full, bf), jax.Sha...  3.71 us

profile of v2, /device:TPU:8, one launch (start us, length us, event | category | flops | bytes accessed | tf_op | source)
XLA Modules:
  0.0 168.6 jit_solution(17322968679290637180)
XLA Ops:
  0.6 164.2 %shard_map.109 = (bf16[8,32,1024]{2,1,0:T(8,128)(2,1)}, bf16[8,32,1024]{2,1,0:T(8,128)(2,1)}, bf16[512,1024]{1,0:T(8,128)(2,1)}, f32[8,128]{1,0:T(8,128)}) custom-call(bf16[8,32,1024]{2,1,0:T(8,128)(2,1)} %bitcast.6, bf16[4,1024,1024]{2,1,0:T(8,128)(2,1)} %bitcast.5, bf16[8,32,1024]{2,1,0:T(8,128)(2,1)} %bitcast.7, f32[1,16]{1,0:T(1,128)} %hist_a.3, ...), custom_call_target="tpu_custom_call" | custom-call | tf_op jit(solution)/shard_map/pallas_call | solution.py:450
  164.8 3.7 %shard_map.110 = (bf16[1,2,128,1024]{3,2,1,0:T(8,128)(2,1)}, bf16[1,2,128,1024]{3,2,1,0:T(8,128)(2,1)}, bf16[1,512,1024]{2,1,0:T(8,128)(2,1)}, f32[1,16]{1,0:T(1...) custom-call(bf16[2,128,1024]{2,1,0:T(8,128)(2,1)} %bitcast.8, bf16[2,128,1024]{2,1,0:T(8,128)(2,1)} %bitcast.9, ...), custom_call_target="tpu_custom_call" | custom-call | tf_op jit(solution)/shard_map/pallas_call | solution.py:485

commit v3 on v2

v3 whole, which is shorter than its diff:
```python
import functools

import jax
import jax.numpy as jnp
from jax import lax
from jax.experimental import pallas as pl
from jax.experimental.pallas import tpu as pltpu
from jax.sharding import PartitionSpec as P

MESH = pl.DeviceIdType.MESH
PIECES = 8
AHEAD = 6
LAG = 2
WARM = 4
UPDATES = ((0, 8), (8, 4), (12, 4))
PAIR = 2
HALVES = 2


def kernel(S, N, T, NC, RC, F, FA,
           acts, weights, cot, hist_a, hist_w, hist_g,
           out_acts, out_grads, out_w, out_top,
           w, wt, x, xq, xo, acc, pt, pr, gin, gout, G, A, dw, dwb, pz, py, amax, gmax,
           w_sem, i_ss, x_ss, x_rs, A_ss, A_rs, B_ss, B_rs, p_ss, p_rs,
           G_ss, G_rs, b_ss, b_rs, z_ss, z_rs, y_ss, y_rs, o_sem, ow_sem):
    s, d, t = lax.axis_index("pipe"), lax.axis_index("dp"), lax.axis_index("tensor")
    last = S - 1
    bf, f32 = jnp.bfloat16, jnp.float32
    upper = s >= S // 2
    wide = s >= last - 1
    tail = LAG * (N // 2)
    level = (s == 0).astype(jnp.int32)
    up = jnp.minimum(s + 1, last)
    down = jnp.maximum(s - 1, 0)
    ratio = N // T
    far_hops = N // 2
    near_hops = N - 1 - far_hops
    offsets = [T // 2] + [o for o in range(1, T) if o != T // 2]

    def remote(src, dst, ss, rsem, **where):
        return pltpu.make_async_remote_copy(
            src_ref=src, dst_ref=dst, send_sem=ss, recv_sem=rsem,
            device_id=where, device_id_type=MESH)

    def peer(o):
        return lax.rem(t + o, T)

    def row(k):
        return lax.rem(d + k, N)

    loads = [pltpu.make_async_copy(weights.at[b], w.at[b], w_sem.at[b]) for b in range(T)]
    for copy in loads:
        copy.start()

    barrier = pltpu.get_barrier_semaphore()
    for k in range(1, N):
        pl.semaphore_signal(barrier, inc=1, device_id={"dp": row(k)}, device_id_type=MESH)
    for o in range(1, T):
        pl.semaphore_signal(barrier, inc=1, device_id={"tensor": peer(o)}, device_id_type=MESH)

    @pl.when(s > 0)
    def _():
        for j in range(T):
            pl.semaphore_signal(barrier, inc=1, device_id={"pipe": s - 1, "tensor": j}, device_id_type=MESH)

    @pl.when(s < last)
    def _():
        for j in range(T):
            pl.semaphore_signal(barrier, inc=1, device_id={"pipe": s + 1, "tensor": j}, device_id_type=MESH)

    lim_a = jnp.max(hist_a[...], axis=1, keepdims=True).astype(bf)
    lim_w = jnp.max(hist_w[...], axis=1, keepdims=True).astype(bf)
    lim_g = jnp.max(hist_g[...], axis=1, keepdims=True).astype(bf)

    def clip(v, lim):
        return jnp.minimum(jnp.maximum(v, -lim), lim)

    def fold(v):
        return jnp.max(jnp.abs(v).reshape(-1, 16, v.shape[-1]), axis=0)

    amax[...] = jnp.zeros_like(amax)
    gmax[...] = jnp.zeros_like(gmax)

    near = (s > 0).astype(jnp.int32) + (s < last).astype(jnp.int32)
    pl.semaphore_wait(barrier, N - 1 + T - 1 + T * near)

    def settled(ref, sem):
        return remote(ref, ref, sem, sem, tensor=peer(1))

    crossing = jnp.logical_and(s > 0, lax.rem(s, 2) == 0)
    crossing_up = lax.rem(s, 2) == 1

    def first_copy(c, o):
        return remote(acts.at[c], x.at[c, t], i_ss, x_rs.at[c, 1], tensor=peer(o))

    def x_copy(c, o, cols):
        lead = jnp.where(crossing_up, T // 2, 0) == o
        return remote(xo.at[c, :, cols], x.at[c, t, :, cols], x_ss,
                      x_rs.at[c, jnp.where(lead, 0, 1)], pipe=up, tensor=peer(o))

    def block_of(e):
        start = lax.rem(e, ratio) * FA
        return lax.div(e, ratio), pl.ds(pl.multiple_of(start, FA), FA)

    def A_copy(c, k):
        e = row(k)
        b, cols = block_of(e)
        return remote(xq.at[c, b, :, cols], A.at[c, d], A_ss, A_rs, dp=e)

    def B_copy(c, o):
        return remote(A.at[c], A.at[c], B_ss, B_rs, tensor=peer(o))

    def p_copy(c, j):
        return remote(pt.at[c, j], pr.at[level, c, t], p_ss, p_rs.at[level, c], pipe=down, tensor=j)

    def back_copy(c):
        return remote(gin.at[c], out_grads.at[c], b_ss, b_rs, pipe=up)

    def turn(c):
        return jnp.where(lax.rem(c, 2) == 0, 1, N - 1)

    def G_copy(c, way, h):
        ahead = turn(c) if way == 0 else N - turn(c)
        r = row((h - 1) * (N - ahead))
        return remote(G.at[c, r], G.at[c, r], G_ss, G_rs.at[c, h - 1], dp=row(ahead))

    def z_copy(k):
        return remote(pz.at[0], pz.at[k], z_ss, z_rs, dp=row(k))

    def y_copy(o):
        return remote(py.at[0], py.at[o], y_ss, y_rs, tensor=peer(o))

    def acts_out(c):
        return pltpu.make_async_copy(xo.at[c], out_acts.at[c], o_sem.at[0])

    def grads_out(c):
        return pltpu.make_async_copy(gout.at[c], out_grads.at[c], o_sem.at[1])

    def each_chunk(body):
        def step(c, _):
            body(c)
            return 0

        lax.fori_loop(0, NC, step, 0)

    def send_first(c):
        for o in offsets:
            first_copy(c, o).start()

    @pl.when(s == 0)
    def _():
        for c in range(AHEAD):
            send_first(c)

        def body(c):
            x[c, t] = acts[c]

        each_chunk(body)

    peak = jnp.zeros((16, F), bf)
    for b in range(T):
        loads[b].wait()

        def squeeze(i, m, b=b):
            rows = pl.ds(pl.multiple_of(i * 128, 128), 128)
            v = w[b, rows]
            w[b, rows] = clip(v, lim_w)
            return jnp.maximum(m, fold(v))

        peak = lax.fori_loop(0, F // 128, squeeze, peak)
    top_w = jnp.max(peak.astype(f32), keepdims=True).reshape(1, 1)
    pz[0] = jnp.broadcast_to(top_w, (8, 128))

    def flip_weights():
        def turn_block(i, _):
            b, n = lax.div(i, F // 128), lax.rem(i, F // 128)
            rows = pl.ds(pl.multiple_of(n * 128, 128), 128)
            wt[b, :, rows] = w[b, rows, :].T
            return 0

        lax.fori_loop(0, T * (F // 128), turn_block, 0)

    pl.when(upper)(flip_weights)

    middle = [o for o in range(1, T) if o != T // 2]

    def forward(c, n):
        first = peer(jnp.where(crossing, T // 2, 0))
        rest = [peer(o) for o in middle] + [peer(jnp.where(crossing, 0, T // 2))]
        span, high = pl.ds(c, n), n * RC

        @pl.when(s > 0)
        def _():
            for m in range(n):
                settled(x.at[c + m, 0], x_rs.at[c + m, 0]).wait_recv()

        q = clip(x[span, first], lim_a)
        xq[span, first] = q
        acc[pl.ds(0, high)] = jnp.dot(q.reshape(high, F), w[first], preferred_element_type=f32)
        for m in range(n):
            settled(x.at[c + m, pl.ds(0, T - 1)], x_rs.at[c + m, 1]).wait_recv()
        for j in rest:
            xq[span, j] = clip(x[span, j], lim_a)
        width = F // HALVES
        for k in range(HALVES):
            cols = pl.ds(k * width, width)
            y = acc[pl.ds(0, high), cols] + x[span, t, :, cols].reshape(high, width).astype(f32)
            for j in rest:
                y = y + jnp.dot(xq[span, j].reshape(high, F), w[j, :, cols], preferred_element_type=f32)
            xo[span, :, cols] = y.astype(bf).reshape(n, RC, width)

            @pl.when(s < last)
            def _():
                for m in range(n):
                    for o in offsets + [0]:
                        x_copy(c + m, o, cols).start()

        if n == 1:
            @pl.when(jnp.logical_and(s == 0, c + AHEAD < NC))
            def _():
                send_first(jnp.minimum(c + AHEAD, NC - 1))

        for m in range(n):
            acts_out(c + m).start()

            @pl.when(lax.rem(c + m, T) == t)
            def _():
                send_A(c + m)
                b, cols = block_of(d)
                A[c + m, d] = xq[c + m, b, :, cols]

        amax[...] = jnp.maximum(amax[...], fold(x[span, t]))

    def send_A(c):
        for k in range(1, N):
            A_copy(c, k).start()

    def backward(c, n):
        span, high = pl.ds(c, n), n * RC

        def last_grads():
            gin[span] = (cot[span].astype(f32) * xo[span].astype(f32)).astype(bf)

        def summed_grads():
            for m in range(n):
                settled(pr.at[0, c + m], p_rs.at[0, c + m]).wait_recv()
            total = pr[0, span, 0].astype(f32)
            for j in range(1, T):
                total = total + pr[0, span, j].astype(f32)
            gin[span] = total.astype(bf)
            for m in range(n):
                back_copy(c + m).start()

        if n == 1:
            summed_grads()
        else:
            pl.when(s == last)(last_grads)
            pl.when(s < last)(summed_grads)
        g = gin[span]
        q = clip(g, lim_g)
        G[span, d] = q
        for m in range(n):
            for way in range(2):
                G_copy(c + m, way, 1).start()
        q = q.reshape(high, F)
        for o in offsets:
            b = peer(o)
            pt[span, b] = jnp.dot(q, wt[b], preferred_element_type=f32).astype(bf).reshape(n, RC, F)
            for m in range(n):
                p_copy(c + m, b).start()
        y = jnp.dot(q, wt[t], preferred_element_type=f32) + g.reshape(high, F).astype(f32)
        pt[span, t] = y.astype(bf).reshape(n, RC, F)

        @pl.when(s > 0)
        def _():
            for m in range(n):
                p_copy(c + m, t).start()

        gmax[...] = jnp.maximum(gmax[...], fold(g))

        @pl.when(c == NC - n)
        def _():
            line = lax.broadcasted_iota(jnp.int32, (8, 128), 0)
            top_a = jnp.max(amax[...].astype(f32), keepdims=True).reshape(1, 1)
            top_g = jnp.max(gmax[...].astype(f32), keepdims=True).reshape(1, 1)
            pz[0] = jnp.where(line == 0, top_a, jnp.where(line == 1, pz[0], top_g))
            for k in range(1, N):
                z_copy(k).start()

    def finish_grads(c):
        settled(pr.at[1, c, pl.ds(0, T - 1)], p_rs.at[1, c]).wait_recv()
        total = pt[c, t].astype(f32)
        for o in range(1, T):
            total = total + pr[1, c, peer(o)].astype(f32)
        gout[c] = total.astype(bf)
        grads_out(c).start()

    def spread():
        settled(A.at[pl.ds(0, NC // T), pl.ds(0, N - 1)], A_rs).wait_recv()
        for m in range(NC // T):
            for o in offsets:
                B_copy(t + T * m, o).start()

    def relay(c, h):
        @pl.when(jnp.logical_and(c >= 0, c < NC))
        def _():
            ways = 2 if h <= near_hops else 1
            settled(G.at[c, pl.ds(0, ways)], G_rs.at[c, h - 1]).wait_recv()
            for way, hops in ((0, far_hops), (1, near_hops)):
                if h < hops:
                    G_copy(c, way, h + 1).start()

    def update(first, count):
        if first == 0:
            settled(A.at[pl.ds(0, NC - NC // T)], B_rs).wait_recv()
        tile, depth = 256, count * N * RC
        span = pl.ds(first, count)

        def body(n, _):
            cols = pl.ds(pl.multiple_of(n * tile, tile), tile)
            y = lax.dot_general(A[span, :, :, cols].reshape(depth, tile), G[span].reshape(depth, F),
                                (((0,), (0,)), ((), ())), preferred_element_type=f32)
            if first:
                y = dw[cols, :] + y
            if first + count < NC:
                dw[cols, :] = y
            else:
                dwb[cols, :] = y.astype(bf)
            return 0

        lax.fori_loop(0, FA // tile, body, 0)

    def after(c):
        for h in range(1, far_hops + 1):
            relay(c - LAG * h, h)

        @pl.when(jnp.logical_and(s == 0, jnp.logical_and(c >= 4, c < NC + 4)))
        def _():
            finish_grads(c - 4)

        @pl.when(jnp.logical_and(upper, c == jnp.where(wide, 4, NC)))
        def _():
            spread()

        @pl.when(c == NC + 1)
        def _():
            settled(pz.at[pl.ds(1, N - 1)], z_rs).wait_recv()
            py[0] = jnp.max(pz[...], axis=0)
            for o in range(1, T):
                y_copy(o).start()

        for first, count in UPDATES:
            @pl.when(c == max(NC, first + count - 1 + tail))
            def _():
                update(first, count)

    count = jnp.where(wide, NC // PAIR, NC)
    warm = jnp.where(s == last, 1, jnp.where(wide, WARM, count))

    def slot(i, _):
        m = i - count
        turned = i - warm
        mixed = jnp.logical_and(turned >= 0, i < 2 * count - warm)
        odd = lax.rem(i + 2 * NC - warm, 2) == 1
        ahead = jnp.logical_or(turned < 0, jnp.logical_and(mixed, odd))
        turn_c = jnp.where(turned < 0, i, jnp.where(mixed, lax.div(turned, 2) + jnp.where(odd, warm, 0), m))
        paired = m < 2 * NC
        even = lax.rem(i + NC, 2) == 0
        is_fwd = jnp.where(wide, jnp.logical_and(ahead, i < 2 * count), i < NC)
        is_bwd = jnp.where(wide, jnp.logical_and(jnp.logical_not(ahead), i < 2 * count),
                           jnp.logical_and(jnp.logical_and(m >= 0, paired), even))
        c_after = jnp.where(wide, i - 2 * count, jnp.where(paired, lax.div(m, 2), m - NC))
        is_after = jnp.logical_and(jnp.logical_not(jnp.logical_or(is_fwd, is_bwd)), c_after < NC + tail)
        c_fwd = jnp.where(wide, turn_c, i)
        c_bwd = jnp.where(wide, turn_c, lax.div(m, 2))

        @pl.when(jnp.logical_and(i == NC, jnp.logical_not(upper)))
        def _():
            flip_weights()
            spread()

        for body, on, c in ((forward, is_fwd, c_fwd), (backward, is_bwd, c_bwd)):
            @pl.when(jnp.logical_and(on, jnp.logical_not(wide)))
            def _():
                body(c, 1)

            @pl.when(jnp.logical_and(on, wide))
            def _():
                body(PAIR * c, PAIR)

        @pl.when(is_after)
        def _():
            after(c_after)

        return 0

    lax.fori_loop(0, 3 * NC + LAG * far_hops, slot, 0)

    out = pltpu.make_async_copy(dwb, out_w, ow_sem)
    out.start()

    settled(py.at[pl.ds(1, T - 1)], y_rs).wait_recv()
    out_top[...] = jnp.max(py[...], axis=0)

    settled(A.at[pl.ds(0, NC // T), pl.ds(0, N - 1)], A_ss).wait_send()
    settled(A.at[pl.ds(0, NC - NC // T)], B_ss).wait_send()
    settled(G.at[:, pl.ds(0, N - 1)], G_ss).wait_send()
    settled(pz.at[pl.ds(1, N - 1)], z_ss).wait_send()
    settled(py.at[pl.ds(1, T - 1)], y_ss).wait_send()
    pltpu.make_async_copy(xo, out_acts, o_sem.at[0]).wait()

    @pl.when(s == 0)
    def _():
        settled(x.at[:, pl.ds(0, T - 1)], i_ss).wait_send()
        settled(pt.at[:, pl.ds(0, T - 1)], p_ss).wait_send()
        pltpu.make_async_copy(gout, out_grads, o_sem.at[1]).wait()

    @pl.when(s > 0)
    def _():
        settled(pt, p_ss).wait_send()
        settled(out_grads, b_rs).wait_recv()

    @pl.when(s < last)
    def _():
        settled(x, x_ss).wait_send()
        settled(gin, b_ss).wait_send()

    out.wait()


def finish(acts, grads, dw, top, hist_a, hist_w, hist_g,
           out_acts, out_grads, out_w, out_ha, out_hw, out_hg, held_a, held_g, held_w, in_sem, out_sem):
    half = dw.shape[0] // 2
    moves = [(acts, held_a, out_acts.at[0]), (grads, held_g, out_grads.at[0])]
    for i in range(2):
        rows = pl.ds(i * half, half)
        moves.append((dw.at[rows], held_w.at[rows], out_w.at[0, rows]))
    inward = [pltpu.make_async_copy(src, held, in_sem.at[0, i]) for i, (src, held, _) in enumerate(moves)]
    outward = [pltpu.make_async_copy(held, dst, out_sem.at[0, i]) for i, (_, held, dst) in enumerate(moves)]
    for copy in inward:
        copy.start()
    peaks = top[...]
    for row, (hist, out_hist) in enumerate(((hist_a, out_ha), (hist_w, out_hw), (hist_g, out_hg))):
        old = hist[...]
        out_hist[...] = jnp.concatenate([peaks[row:row + 1, 0:1], old[:, :-1]], axis=1)
    for copy, onward in zip(inward, outward):
        copy.wait()
        onward.start()
    for onward in outward:
        onward.wait()


def shards(acts_in, weights, cotangent, hist_act, hist_weight, hist_grad):
    S, N, T = lax.axis_size("pipe"), lax.axis_size("dp"), lax.axis_size("tensor")
    M, R, F = acts_in.shape
    NC, RC = M * PIECES, R // PIECES
    FA = T * F // N
    bf, f32 = jnp.bfloat16, jnp.float32
    dma = pltpu.SemaphoreType.DMA
    vmem = pl.BlockSpec(memory_space=pltpu.VMEM)
    anyw = pl.BlockSpec(memory_space=pl.ANY)
    hist = jax.ShapeDtypeStruct(hist_act.shape, f32)
    chunk = (NC, RC, F)
    acts, grads, dw, top = pl.pallas_call(
        functools.partial(kernel, S, N, T, NC, RC, F, FA),
        out_shape=(jax.ShapeDtypeStruct(chunk, bf), jax.ShapeDtypeStruct(chunk, bf),
                   jax.ShapeDtypeStruct((FA, F), bf), jax.ShapeDtypeStruct((8, 128), f32)),
        in_specs=[vmem, anyw, vmem, vmem, vmem, vmem],
        out_specs=(anyw, anyw, anyw, vmem),
        scratch_shapes=[
            pltpu.VMEM((T, F, F), bf),
            pltpu.VMEM((T, F, F), bf),
            pltpu.VMEM((NC, T, RC, F), bf),
            pltpu.VMEM((NC, T, RC, F), bf),
            pltpu.VMEM(chunk, bf),
            pltpu.VMEM((PAIR * RC, F), f32),
            pltpu.VMEM((NC, T, RC, F), bf),
            pltpu.VMEM((2, NC, T, RC, F), bf),
            pltpu.VMEM(chunk, bf),
            pltpu.VMEM(chunk, bf),
            pltpu.VMEM((NC, N, RC, F), bf),
            pltpu.VMEM((NC, N, RC, FA), bf),
            pltpu.VMEM((FA, F), f32),
            pltpu.VMEM((FA, F), bf),
            pltpu.VMEM((N, 8, 128), f32),
            pltpu.VMEM((T, 8, 128), f32),
            pltpu.VMEM((16, F), bf),
            pltpu.VMEM((16, F), bf),
            dma((T,)), dma(()), dma(()), dma((NC, 2)), dma(()), dma(()), dma(()), dma(()),
            dma(()), dma((2, NC)), dma(()), dma((NC, N // 2)), dma(()), dma(()),
            dma(()), dma(()), dma(()), dma(()), dma((2,)), dma(()),
        ],
        compiler_params=pltpu.CompilerParams(
            collective_id=0, has_side_effects=True, vmem_limit_bytes=60 * 2**20),
    )(acts_in.reshape(chunk), weights.reshape(T, F, F), cotangent.reshape(chunk),
      hist_act, hist_weight, hist_grad)
    full = (1, M, R, F)
    return pl.pallas_call(
        finish,
        out_shape=(jax.ShapeDtypeStruct(full, bf), jax.ShapeDtypeStruct(full, bf),
                   jax.ShapeDtypeStruct((1, FA, F), bf), hist, hist, hist),
        in_specs=[anyw, anyw, anyw, vmem, vmem, vmem, vmem],
        out_specs=(anyw, anyw, anyw, vmem, vmem, vmem),
        scratch_shapes=[pltpu.VMEM((M, R, F), bf), pltpu.VMEM((M, R, F), bf),
                        pltpu.VMEM((FA, F), bf), dma((2, 4)), dma((2, 4))],
        compiler_params=pltpu.CompilerParams(vmem_limit_bytes=60 * 2**20),
    )(acts.reshape(M, R, F), grads.reshape(M, R, F), dw, top, hist_act, hist_weight, hist_grad)


def solution(mesh):
    placed = (P(None, "dp", "tensor"), P("pipe", None, "tensor"), P(None, "dp", "tensor"),
              P("pipe", None), P("pipe", None), P("pipe", None))
    return jax.shard_map(
        shards, mesh=mesh, in_specs=placed,
        out_specs=(P("pipe", None, "dp", "tensor"), P("pipe", None, "dp", "tensor"),
                   P("pipe", "dp", "tensor"), P("pipe", None), P("pipe", None), P("pipe", None)),
        check_vma=False)
```

time: 169 us -> 149 us (0.88)
  Pallas kernels: 168 us -> 147 us
    pallas_call x1, Pallas kernels: 164 us -> 143 us  [shards(): pl.pallas_call(functools.partial(kernel, S, N, T, NC, RC, F, FA), out_sha...]
where the time goes in v3:
time: 149 us; the launch traced here: 148 us
  Pallas kernels  147 us (99%)
    pallas_call x1, Pallas kernels, shards(): pl.pallas_call(functools.partial(kernel, S, N, T, NC, RC, F, FA), out_sha...  143 us
    pallas_call x1, Pallas kernels, shards(): pl.pallas_call(finish, out_shape=(jax.ShapeDtypeStruct(full, bf), jax.Sha...  3.71 us

profile of v3, /device:TPU:8, one launch (start us, length us, event | category | flops | bytes accessed | tf_op | source)
XLA Modules:
  0.0 147.8 jit_solution(17397905979868275351)
XLA Ops:
  0.6 143.4 %shard_map.109 = (bf16[16,16,1024]{2,1,0:T(8,128)(2,1)}, bf16[16,16,1024]{2,1,0:T(8,128)(2,1)}, bf16[512,1024]{1,0:T(8,128)(2,1)}, f32[8,128]{1,0:T(8,128)}) custom-call(bf16[16,16,1024]{2,1,0:T(8,128)(2,1)} %bitcast.6, bf16[4,1024,1024]{2,1,0:T(8,128)(2,1)} %bitcast.5, bf16[16,16,1024]{2,1,0:T(8,128)(2,1)} %bitcast.7, f32[1,16]{1,0:T(1,128)} %hist_a.3, ...), custom_call_target="tpu_custom_call" | custom-call | tf_op jit(solution)/shard_map/pallas_call | solution.py:464
  144.1 3.7 %shard_map.110 = (bf16[1,2,128,1024]{3,2,1,0:T(8,128)(2,1)}, bf16[1,2,128,1024]{3,2,1,0:T(8,128)(2,1)}, bf16[1,512,1024]{2,1,0:T(8,128)(2,1)}, f32[1,16]{1,0:T(1...) custom-call(bf16[2,128,1024]{2,1,0:T(8,128)(2,1)} %bitcast.8, bf16[2,128,1024]{2,1,0:T(8,128)(2,1)} %bitcast.9, ...), custom_call_target="tpu_custom_call" | custom-call | tf_op jit(solution)/shard_map/pallas_call | solution.py:498

commit v4 on v3

--- a/solution.py
+++ b/solution.py
@@ -10,7 +10,8 @@
 MESH = pl.DeviceIdType.MESH
 PIECES = 8
 AHEAD = 6
-LAG = 2
+LAG_LOW, LAG_HIGH = 2, 3
+CUTS = 4
 WARM = 4
 UPDATES = ((0, 8), (8, 4), (12, 4))
 PAIR = 2
@@ -18,18 +19,18 @@
 
 
 def kernel(S, N, T, NC, RC, F, FA,
-           acts, weights, cot, hist_a, hist_w, hist_g,
+           acts_in, weights, cot_in, hists_a, hists_w, hists_g,
            out_acts, out_grads, out_w, out_top,
-           w, wt, x, xq, xo, acc, pt, pr, gin, gout, G, A, dw, dwb, pz, py, amax, gmax,
-           w_sem, i_ss, x_ss, x_rs, A_ss, A_rs, B_ss, B_rs, p_ss, p_rs,
+           acts, cot, hist_a, hist_w, hist_g, w, wt, x, xq, xo, acc, pt, pr, gin, gout, G, A, dw, dwb, pz, py, amax, gmax,
+           in_sem, w_sem, i_ss, x_ss, x_rs, A_ss, A_rs, B_ss, B_rs, p_ss, p_rs, f_rs,
            G_ss, G_rs, b_ss, b_rs, z_ss, z_rs, y_ss, y_rs, o_sem, ow_sem):
     s, d, t = lax.axis_index("pipe"), lax.axis_index("dp"), lax.axis_index("tensor")
     last = S - 1
     bf, f32 = jnp.bfloat16, jnp.float32
     upper = s >= S // 2
     wide = s >= last - 1
-    tail = LAG * (N // 2)
-    level = (s == 0).astype(jnp.int32)
+    lag = jnp.where(s < 2, LAG_LOW, LAG_HIGH)
+    tail = lag * (N // 2)
     up = jnp.minimum(s + 1, last)
     down = jnp.maximum(s - 1, 0)
     ratio = N // T
@@ -48,10 +49,6 @@
     def row(k):
         return lax.rem(d + k, N)
 
-    loads = [pltpu.make_async_copy(weights.at[b], w.at[b], w_sem.at[b]) for b in range(T)]
-    for copy in loads:
-        copy.start()
-
     barrier = pltpu.get_barrier_semaphore()
     for k in range(1, N):
         pl.semaphore_signal(barrier, inc=1, device_id={"dp": row(k)}, device_id_type=MESH)
@@ -68,6 +65,19 @@
         for j in range(T):
             pl.semaphore_signal(barrier, inc=1, device_id={"pipe": s + 1, "tensor": j}, device_id_type=MESH)
 
+    fills = [pltpu.make_async_copy(src, dst, in_sem.at[i]) for i, (src, dst) in enumerate((
+        (hists_a, hist_a), (hists_w, hist_w), (hists_g, hist_g), (acts_in, acts), (cot_in, cot)))]
+    for copy in fills:
+        copy.start()
+    loads = [pltpu.make_async_copy(weights.at[b], w.at[b], w_sem.at[b]) for b in range(T)]
+    for copy in loads:
+        copy.start()
+
+    amax[...] = jnp.zeros_like(amax)
+    gmax[...] = jnp.zeros_like(gmax)
+    for copy in fills:
+        copy.wait()
+
     lim_a = jnp.max(hist_a[...], axis=1, keepdims=True).astype(bf)
     lim_w = jnp.max(hist_w[...], axis=1, keepdims=True).astype(bf)
     lim_g = jnp.max(hist_g[...], axis=1, keepdims=True).astype(bf)
@@ -77,9 +87,6 @@
 
     def fold(v):
         return jnp.max(jnp.abs(v).reshape(-1, 16, v.shape[-1]), axis=0)
-
-    amax[...] = jnp.zeros_like(amax)
-    gmax[...] = jnp.zeros_like(gmax)
 
     near = (s > 0).astype(jnp.int32) + (s < last).astype(jnp.int32)
     pl.semaphore_wait(barrier, N - 1 + T - 1 + T * near)
@@ -111,7 +118,10 @@
         return remote(A.at[c], A.at[c], B_ss, B_rs, tensor=peer(o))
 
     def p_copy(c, j):
-        return remote(pt.at[c, j], pr.at[level, c, t], p_ss, p_rs.at[level, c], pipe=down, tensor=j)
+        return remote(pt.at[c, j], pr.at[0, c, t], p_ss, p_rs.at[c], pipe=down, tensor=j)
+
+    def f_copy(c, o):
+        return remote(pt.at[c, peer(o)], pr.at[1, c, t], p_ss, f_rs, tensor=peer(o))
 
     def back_copy(c):
         return remote(gin.at[c], out_grads.at[c], b_ss, b_rs, pipe=up)
@@ -133,8 +143,7 @@
     def acts_out(c):
         return pltpu.make_async_copy(xo.at[c], out_acts.at[c], o_sem.at[0])
 
-    def grads_out(c):
-        return pltpu.make_async_copy(gout.at[c], out_grads.at[c], o_sem.at[1])
+    grads_out = pltpu.make_async_copy(gout, out_grads, o_sem.at[1])
 
     def each_chunk(body):
         def step(c, _):
@@ -243,7 +252,7 @@
 
         def summed_grads():
             for m in range(n):
-                settled(pr.at[0, c + m], p_rs.at[0, c + m]).wait_recv()
+                settled(pr.at[0, c + m], p_rs.at[c + m]).wait_recv()
             total = pr[0, span, 0].astype(f32)
             for j in range(1, T):
                 total = total + pr[0, span, j].astype(f32)
@@ -263,18 +272,25 @@
             for way in range(2):
                 G_copy(c + m, way, 1).start()
         q = q.reshape(high, F)
-        for o in offsets:
-            b = peer(o)
-            pt[span, b] = jnp.dot(q, wt[b], preferred_element_type=f32).astype(bf).reshape(n, RC, F)
-            for m in range(n):
-                p_copy(c + m, b).start()
-        y = jnp.dot(q, wt[t], preferred_element_type=f32) + g.reshape(high, F).astype(f32)
-        pt[span, t] = y.astype(bf).reshape(n, RC, F)
-
-        @pl.when(s > 0)
-        def _():
-            for m in range(n):
-                p_copy(c + m, t).start()
+        for group in (offsets[:2], offsets[2:] + [0]):
+            for o in group:
+                y = jnp.dot(q, wt[peer(o)], preferred_element_type=f32)
+                if o == 0:
+                    y = y + g.reshape(high, F).astype(f32)
+                pt[span, peer(o)] = y.astype(bf).reshape(n, RC, F)
+
+            @pl.when(s > 0)
+            def _():
+                for o in group:
+                    for m in range(n):
+                        p_copy(c + m, peer(o)).start()
+
+            if n == 1:
+                @pl.when(s == 0)
+                def _():
+                    for o in group:
+                        if o:
+                            f_copy(c, o).start()
 
         gmax[...] = jnp.maximum(gmax[...], fold(g))
 
@@ -287,13 +303,17 @@
             for k in range(1, N):
                 z_copy(k).start()
 
-    def finish_grads(c):
-        settled(pr.at[1, c, pl.ds(0, T - 1)], p_rs.at[1, c]).wait_recv()
-        total = pt[c, t].astype(f32)
-        for o in range(1, T):
-            total = total + pr[1, c, peer(o)].astype(f32)
-        gout[c] = total.astype(bf)
-        grads_out(c).start()
+    def finish_grads():
+        settled(pr.at[1, :, pl.ds(0, T - 1)], f_rs).wait_recv()
+
+        def body(c):
+            total = pt[c, t].astype(f32)
+            for o in range(1, T):
+                total = total + pr[1, c, peer(o)].astype(f32)
+            gout[c] = total.astype(bf)
+
+        each_chunk(body)
+        grads_out.start()
 
     def spread():
         settled(A.at[pl.ds(0, NC // T), pl.ds(0, N - 1)], A_rs).wait_recv()
@@ -326,17 +346,18 @@
                 dw[cols, :] = y
             else:
                 dwb[cols, :] = y.astype(bf)
+                pltpu.make_async_copy(dwb.at[cols], out_w.at[cols], ow_sem).start()
             return 0
 
         lax.fori_loop(0, FA // tile, body, 0)
 
     def after(c):
         for h in range(1, far_hops + 1):
-            relay(c - LAG * h, h)
-
-        @pl.when(jnp.logical_and(s == 0, jnp.logical_and(c >= 4, c < NC + 4)))
-        def _():
-            finish_grads(c - 4)
+            relay(c - lag * h, h)
+
+        @pl.when(jnp.logical_and(s == 0, c == NC + 2))
+        def _():
+            finish_grads()
 
         @pl.when(jnp.logical_and(upper, c == jnp.where(wide, 4, NC)))
         def _():
@@ -350,7 +371,7 @@
                 y_copy(o).start()
 
         for first, count in UPDATES:
-            @pl.when(c == max(NC, first + count - 1 + tail))
+            @pl.when(c == first + count - 1 + tail)
             def _():
                 update(first, count)
 
@@ -394,10 +415,7 @@
 
         return 0
 
-    lax.fori_loop(0, 3 * NC + LAG * far_hops, slot, 0)
-
-    out = pltpu.make_async_copy(dwb, out_w, ow_sem)
-    out.start()
+    lax.fori_loop(0, 3 * NC + far_hops * max(LAG_LOW, LAG_HIGH), slot, 0)
 
     settled(py.at[pl.ds(1, T - 1)], y_rs).wait_recv()
     out_top[...] = jnp.max(py[...], axis=0)
@@ -413,7 +431,7 @@
     def _():
         settled(x.at[:, pl.ds(0, T - 1)], i_ss).wait_send()
         settled(pt.at[:, pl.ds(0, T - 1)], p_ss).wait_send()
-        pltpu.make_async_copy(gout, out_grads, o_sem.at[1]).wait()
+        grads_out.wait()
 
     @pl.when(s > 0)
     def _():
@@ -425,18 +443,18 @@
         settled(x, x_ss).wait_send()
         settled(gin, b_ss).wait_send()
 
-    out.wait()
+    pltpu.make_async_copy(dwb, out_w, ow_sem).wait()
 
 
 def finish(acts, grads, dw, top, hist_a, hist_w, hist_g,
            out_acts, out_grads, out_w, out_ha, out_hw, out_hg, held_a, held_g, held_w, in_sem, out_sem):
-    half = dw.shape[0] // 2
     moves = [(acts, held_a, out_acts.at[0]), (grads, held_g, out_grads.at[0])]
-    for i in range(2):
-        rows = pl.ds(i * half, half)
+    part = dw.shape[0] // CUTS
+    for i in range(CUTS):
+        rows = pl.ds(i * part, part)
         moves.append((dw.at[rows], held_w.at[rows], out_w.at[0, rows]))
-    inward = [pltpu.make_async_copy(src, held, in_sem.at[0, i]) for i, (src, held, _) in enumerate(moves)]
-    outward = [pltpu.make_async_copy(held, dst, out_sem.at[0, i]) for i, (_, held, dst) in enumerate(moves)]
+    inward = [pltpu.make_async_copy(src, held, in_sem.at[i]) for i, (src, held, _) in enumerate(moves)]
+    outward = [pltpu.make_async_copy(held, dst, out_sem.at[i]) for i, (_, held, dst) in enumerate(moves)]
     for copy in inward:
         copy.start()
     peaks = top[...]
@@ -459,15 +477,21 @@
     dma = pltpu.SemaphoreType.DMA
     vmem = pl.BlockSpec(memory_space=pltpu.VMEM)
     anyw = pl.BlockSpec(memory_space=pl.ANY)
+    hbm = pl.BlockSpec(memory_space=pltpu.HBM)
     hist = jax.ShapeDtypeStruct(hist_act.shape, f32)
     chunk = (NC, RC, F)
     acts, grads, dw, top = pl.pallas_call(
         functools.partial(kernel, S, N, T, NC, RC, F, FA),
         out_shape=(jax.ShapeDtypeStruct(chunk, bf), jax.ShapeDtypeStruct(chunk, bf),
                    jax.ShapeDtypeStruct((FA, F), bf), jax.ShapeDtypeStruct((8, 128), f32)),
-        in_specs=[vmem, anyw, vmem, vmem, vmem, vmem],
+        in_specs=[hbm] * 6,
         out_specs=(anyw, anyw, anyw, vmem),
         scratch_shapes=[
+            pltpu.VMEM(chunk, bf),
+            pltpu.VMEM(chunk, bf),
+            pltpu.VMEM(hist_act.shape, f32),
+            pltpu.VMEM(hist_act.shape, f32),
+            pltpu.VMEM(hist_act.shape, f32),
             pltpu.VMEM((T, F, F), bf),
             pltpu.VMEM((T, F, F), bf),
             pltpu.VMEM((NC, T, RC, F), bf),
@@ -486,8 +510,8 @@
             pltpu.VMEM((T, 8, 128), f32),
             pltpu.VMEM((16, F), bf),
             pltpu.VMEM((16, F), bf),
-            dma((T,)), dma(()), dma(()), dma((NC, 2)), dma(()), dma(()), dma(()), dma(()),
-            dma(()), dma((2, NC)), dma(()), dma((NC, N // 2)), dma(()), dma(()),
+            dma((5,)), dma((T,)), dma(()), dma(()), dma((NC, 2)), dma(()), dma(()), dma(()), dma(()),
+            dma(()), dma((NC,)), dma(()), dma(()), dma((NC, N // 2)), dma(()), dma(()),
             dma(()), dma(()), dma(()), dma(()), dma((2,)), dma(()),
         ],
         compiler_params=pltpu.CompilerParams(
@@ -502,7 +526,7 @@
         in_specs=[anyw, anyw, anyw, vmem, vmem, vmem, vmem],
         out_specs=(anyw, anyw, anyw, vmem, vmem, vmem),
         scratch_shapes=[pltpu.VMEM((M, R, F), bf), pltpu.VMEM((M, R, F), bf),
-                        pltpu.VMEM((FA, F), bf), dma((2, 4)), dma((2, 4))],
+                        pltpu.VMEM((FA, F), bf), dma((2 + CUTS,)), dma((2 + CUTS,))],
         compiler_params=pltpu.CompilerParams(vmem_limit_bytes=60 * 2**20),
     )(acts.reshape(M, R, F), grads.reshape(M, R, F), dw, top, hist_act, hist_weight, hist_grad)
 

time: 149 us -> 147 us (0.987)
  no operation moved by 1% of the time
where the time goes in v4:
time: 147 us
  Pallas kernels  146 us (99%)
    pallas_call x1, Pallas kernels, shards(): pl.pallas_call(functools.partial(kernel, S, N, T, NC, RC, F, FA), out_sha...  142 us
    pallas_call x1, Pallas kernels, shards(): pl.pallas_call(finish, out_shape=(jax.ShapeDtypeStruct(full, bf), jax.Sha...  3.67 us

profile of v4, /device:TPU:8, one launch (start us, length us, event | category | flops | bytes accessed | tf_op | source)
XLA Modules:
  0.0 146.7 jit_solution(11542542611910953081)
XLA Ops:
  0.6 142.4 %shard_map.109 = (bf16[16,16,1024]{2,1,0:T(8,128)(2,1)}, bf16[16,16,1024]{2,1,0:T(8,128)(2,1)}, bf16[512,1024]{1,0:T(8,128)(2,1)}, f32[8,128]{1,0:T(8,128)}) custom-call(bf16[16,16,1024]{2,1,0:T(8,128)(2,1)} %bitcast.6, bf16[4,1024,1024]{2,1,0:T(8,128)(2,1)} %bitcast.5, bf16[16,16,1024]{2,1,0:T(8,128)(2,1)} %bitcast.7, f32[1,16]{1,0:T(1,128)} %hist_a.1, ...), custom_call_target="tpu_custom_call" | custom-call | tf_op jit(solution)/shard_map/pallas_call | solution.py:483
  143.0 3.7 %shard_map.110 = (bf16[1,2,128,1024]{3,2,1,0:T(8,128)(2,1)}, bf16[1,2,128,1024]{3,2,1,0:T(8,128)(2,1)}, bf16[1,512,1024]{2,1,0:T(8,128)(2,1)}, f32[1,16]{1,0:T(1...) custom-call(bf16[2,128,1024]{2,1,0:T(8,128)(2,1)} %bitcast.8, bf16[2,128,1024]{2,1,0:T(8,128)(2,1)} %bitcast.9, ...), custom_call_target="tpu_custom_call" | custom-call | tf_op jit(solution)/shard_map/pallas_call | solution.py:522
